TPU v7x, 256 devices: a whole 4x4x8 slice. The times are simulated.
256 devices in a mesh: trial: 2 (over core), qa: 16 (over y, x), qb: 8 (over z).
Axes of the slice: x: 4, y: 4, z: 8, core: 2. Of those that a mesh axis runs over, the one named last changes fastest.
Arguments:
- wave_parts: float32 [4, 512, 128, 128], P('trial', ('qa', 'qb')), parts along dimension 0, may hold values from -6 to 6
- level_table: float32 [1024, 128, 128], P(('trial', 'qa', 'qb')), parts along dimension 0, may hold values from -2 to 2
- diagonal_angles: float32 [6, 128], P('trial'), parts along dimension 0, may hold values from 0.3 to 1.2
- turn_angles: float32 [6, 4], P('trial'), parts along dimension 0, may hold values from 0.3 to 1.2
Outputs:
- final_parts: float32 [4, 512, 128, 128], P('trial', ('qa', 'qb')), parts along dimension 0
There are 2 independent parts, one for each index of `trial`. A program takes and returns all parts, laid end to end along the dimension named above; each array names one. Nothing has to cross between parts.
All inputs are finite; a program needn't handle non-finite values.
Results may differ from a plain program's by a relative error of at most 0.0003.
Values sent between devices are 32-bit elements.
A program may use at most 64 MiB of HBM per device.

v0:
```python
import jax
import jax.numpy as jnp
from jax import lax
from jax.sharding import PartitionSpec as P

LAYERS = 3


def count_bits(values, count):
    places = jnp.arange(count.bit_length() - 1, dtype=jnp.int32)
    return jnp.sum(values[..., None] >> places & 1, axis=-1)


def rotation_table(count, angle):
    rank = jnp.arange(count, dtype=jnp.int32)
    apart = count_bits(rank[:, None] ^ rank[None, :], count)
    bits = count.bit_length() - 1
    size = jnp.cos(angle) ** (bits - apart).astype(jnp.float32) * jnp.sin(angle) ** apart.astype(
        jnp.float32
    )
    real_sign = jnp.where(apart % 4 == 0, 1.0, jnp.where(apart % 4 == 2, -1.0, 0.0)).astype(
        jnp.float32
    )
    imag_sign = jnp.where(apart % 4 == 1, -1.0, jnp.where(apart % 4 == 3, 1.0, 0.0)).astype(
        jnp.float32
    )
    return (size * real_sign, size * imag_sign)


def mix_dim(values, dim, angle):
    real_part, imag_part = rotation_table(values.shape[dim], angle)

    def times(table):
        moved = jnp.tensordot(values, table, axes=([dim], [0]), precision=lax.Precision.HIGHEST)
        return jnp.moveaxis(moved, -1, dim)

    by_real = times(real_part)
    by_imag = times(imag_part)
    return jnp.stack([by_real[0] - by_imag[1], by_real[1] + by_imag[0]])


def phase_step(values, levels, angle):
    turn = angle * levels
    return jnp.stack(
        [
            values[0] * jnp.cos(turn) + values[1] * jnp.sin(turn),
            values[1] * jnp.cos(turn) - values[0] * jnp.sin(turn),
        ]
    )


def shards(wave_parts, level_table, diagonal_angles, turn_angles):
    values = wave_parts
    for layer in range(LAYERS):
        values = phase_step(values, level_table, diagonal_angles[layer])
        values = mix_dim(values, 3, turn_angles[layer, 0])
        values = mix_dim(values, 2, turn_angles[layer, 1])
        moved = lax.all_to_all(values, "qa", split_axis=2, concat_axis=1, tiled=True)
        moved = mix_dim(moved, 1, turn_angles[layer, 2])
        values = lax.all_to_all(moved, "qa", split_axis=1, concat_axis=2, tiled=True)
        moved = lax.all_to_all(values, "qb", split_axis=3, concat_axis=1, tiled=True)
        spread = moved.reshape(2, lax.axis_size("qb"), -1, moved.shape[2], moved.shape[3])
        moved = mix_dim(spread, 1, turn_angles[layer, 3]).reshape(moved.shape)
        values = lax.all_to_all(moved, "qb", split_axis=1, concat_axis=3, tiled=True)
    return values


def solution(mesh):
    placed = (
        P("trial", ("qa", "qb"), None, None),
        P(("trial", "qa", "qb"), None, None),
        P("trial", None),
        P("trial", None),
    )
    return jax.shard_map(
        shards,
        mesh=mesh,
        in_specs=placed,
        out_specs=P("trial", ("qa", "qb"), None, None),
        check_vma=False,
    )
```

profile of v0, /device:TPU:2, one launch (start us, length us, event | category | flops | bytes accessed | tf_op | source)
XLA Modules:
  0.0 238.1 jit_solution(5712961371041318198)
XLA Ops:
  0.0 1.8 fusion.327
  3.2 0.6 copy-done.1
  3.8 2.0 fusion.19
  5.9 0.8 fusion.17
  6.7 0.8 fusion.16
  9.0 1.1 convolution_bitcast_fusion.17
  10.1 1.1 convolution_bitcast_fusion.16
  11.3 1.0 copy.169
  12.3 7.5 %all-to-all-start = ((f32[2,4,128,128]{3,1,0,2:T(4,128)}), f32[2,4,128,128]{3,1,0,2:T(4,128)S(1)}, u32[]{:S(2)}, u32[]{:S(2)}) async-start(f32[2,4,128,128]{3,1,0,2:T(4,128)} %copy.169), calls=%async_computation | async-start | bytes 1048576 | tf_op jit(solution)/shard_map/all_to_all | solution.py:58
  21.3 8.6 %all-to-all-done = f32[2,4,128,128]{3,1,0,2:T(4,128)S(1)} async-done(((f32[2,4,128,128]{3,1,0,2:T(4,128)}), f32[2,4,128,128]{3,1,0,2:T(4,128)S(1)}, u32[]{:S(2)}, u32[]{:S(2)}) %all-to-all-start) | async-done | bytes 524320 | tf_op jit(solution)/shard_map/all_to_all | solution.py:58
  30.0 0.3 copy.171
  30.4 0.7 convolution_bitcast_fusion.15
  31.1 0.7 convolution_bitcast_fusion.14
  31.9 0.3 copy.174
  32.3 13.8 %all_to_all.201 = f32[2,64,8,128]{3,2,0,1:T(8,128)S(1)} all-to-all(f32[2,64,8,128]{3,2,0,1:T(8,128)S(1)} %copy.174), channel_id=1, replica_groups=mesh['trial'=2,'qa'=16,'qb'=8] {'qa'}, dimensions={1} | all-to-all | bytes 1048576 | tf_op jit(solution)/shard_map/all_to_all | solution.py:60
  46.1 1.0 copy.177
  47.0 8.4 %all-to-all-start.2 = ((f32[2,4,128,128]{2,1,0,3:T(4,128)}), f32[2,4,128,128]{2,1,0,3:T(4,128)S(1)}, u32[]{:S(2)}, u32[]{:S(2)}) async-start(f32[2,4,128,128]{2,1,0,3:T(4,128)} %copy.177), calls=%async_computation.2 | async-start | bytes 1048576 | tf_op jit(solution)/shard_map/all_to_all | solution.py:61
  57.0 14.2 %all-to-all-done.2 = f32[2,4,128,128]{2,1,0,3:T(4,128)S(1)} async-done(((f32[2,4,128,128]{2,1,0,3:T(4,128)}), f32[2,4,128,128]{2,1,0,3:T(4,128)S(1)}, u32[]{:S(2)}, u32[]{:S(2)}) %all-to-all-start.2) | async-done | bytes 524320 | tf_op jit(solution)/shard_map/all_to_all | solution.py:61
  71.2 0.9 convolution_bitcast_fusion.13
  72.1 0.9 convolution_bitcast_fusion.12
  73.2 0.9 copy.184
  74.1 3.7 %all-to-all-start.3 = ((f32[2,32,128,16]{2,3,0,1:T(8,128)}), f32[2,32,128,16]{2,3,0,1:T(8,128)S(1)}, u32[]{:S(2)}, u32[]{:S(2)}) async-start(f32[2,32,128,16]{2,3,0,1:T(8,128)} %copy.184), calls=%async_computation.3 | async-start | bytes 1048576 | tf_op jit(solution)/shard_map/all_to_all | solution.py:64
  80.4 11.2 %all-to-all-done.3 = f32[2,32,128,16]{2,3,0,1:T(8,128)S(1)} async-done(((f32[2,32,128,16]{2,3,0,1:T(8,128)}), f32[2,32,128,16]{2,3,0,1:T(8,128)S(1)}, u32[]{:S(2)}, u32[]{:S(2)}) %all-to-all-start.3) | async-done | bytes 524320 | tf_op jit(solution)/shard_map/all_to_all | solution.py:64
  92.0 0.8 copy-done
  92.8 1.0 add_bitcast_fusion.1
  93.8 0.8 fusion.15
  94.6 0.8 fusion.14
  95.4 1.1 convolution_bitcast_fusion.11
  96.5 1.1 convolution_bitcast_fusion.10
  97.7 1.0 copy.194
  98.7 5.1 %all-to-all-start.4 = ((f32[2,4,128,128]{3,1,0,2:T(4,128)}), f32[2,4,128,128]{3,1,0,2:T(4,128)S(1)}, u32[]{:S(2)}, u32[]{:S(2)}) async-start(f32[2,4,128,128]{3,1,0,2:T(4,128)} %copy.194), calls=%async_computation.4 | async-start | bytes 1048576 | tf_op jit(solution)/shard_map/all_to_all | solution.py:58
  105.2 7.4 %all-to-all-done.4 = f32[2,4,128,128]{3,1,0,2:T(4,128)S(1)} async-done(((f32[2,4,128,128]{3,1,0,2:T(4,128)}), f32[2,4,128,128]{3,1,0,2:T(4,128)S(1)}, u32[]{:S(2)}, u32[]{:S(2)}) %all-to-all-start.4) | async-done | bytes 524320 | tf_op jit(solution)/shard_map/all_to_all | solution.py:58
  112.7 0.3 copy.196
  113.0 0.7 convolution_bitcast_fusion.9
  113.7 0.7 convolution_bitcast_fusion.8
  114.9 13.1 %all_to_all.202 = f32[2,64,8,128]{3,2,0,1:T(8,128)S(1)} all-to-all(f32[2,64,8,128]{3,2,0,1:T(8,128)S(1)} %copy.199), channel_id=1, replica_groups=mesh['trial'=2,'qa'=16,'qb'=8] {'qa'}, dimensions={1} | all-to-all | bytes 1048576 | tf_op jit(solution)/shard_map/all_to_all | solution.py:60
  128.1 1.0 copy.202
  129.1 3.5 %all-to-all-start.6 = ((f32[2,4,128,128]{2,1,0,3:T(4,128)}), f32[2,4,128,128]{2,1,0,3:T(4,128)S(1)}, u32[]{:S(2)}, u32[]{:S(2)}) async-start(f32[2,4,128,128]{2,1,0,3:T(4,128)} %copy.202), calls=%async_computation.6 | async-start | bytes 1048576 | tf_op jit(solution)/shard_map/all_to_all | solution.py:61
  133.9 11.9 %all-to-all-done.6 = f32[2,4,128,128]{2,1,0,3:T(4,128)S(1)} async-done(((f32[2,4,128,128]{2,1,0,3:T(4,128)}), f32[2,4,128,128]{2,1,0,3:T(4,128)S(1)}, u32[]{:S(2)}, u32[]{:S(2)}) %all-to-all-start.6) | async-done | bytes 524320 | tf_op jit(solution)/shard_map/all_to_all | solution.py:61
  145.8 0.9 convolution_bitcast_fusion.7
  146.7 0.9 convolution_bitcast_fusion.6
  147.8 0.9 copy.209
  148.7 3.7 %all-to-all-start.7 = ((f32[2,32,128,16]{2,3,0,1:T(8,128)}), f32[2,32,128,16]{2,3,0,1:T(8,128)S(1)}, u32[]{:S(2)}, u32[]{:S(2)}) async-start(f32[2,32,128,16]{2,3,0,1:T(8,128)} %copy.209), calls=%async_computation.7 | async-start | bytes 1048576 | tf_op jit(solution)/shard_map/all_to_all | solution.py:64
  155.3 10.1 %all-to-all-done.7 = f32[2,32,128,16]{2,3,0,1:T(8,128)S(1)} async-done(((f32[2,32,128,16]{2,3,0,1:T(8,128)}), f32[2,32,128,16]{2,3,0,1:T(8,128)S(1)}, u32[]{:S(2)}, u32[]{:S(2)}) %all-to-all-start.7) | async-done | bytes 524320 | tf_op jit(solution)/shard_map/all_to_all | solution.py:64
  165.8 1.0 add_bitcast_fusion
  166.8 0.8 fusion.13
  167.6 0.8 fusion.12
  168.4 1.1 convolution_bitcast_fusion.5
  169.6 1.1 convolution_bitcast_fusion.4
  170.8 1.0 copy.219
  171.8 4.8 %all-to-all-start.8 = ((f32[2,4,128,128]{3,1,0,2:T(4,128)}), f32[2,4,128,128]{3,1,0,2:T(4,128)S(1)}, u32[]{:S(2)}, u32[]{:S(2)}) async-start(f32[2,4,128,128]{3,1,0,2:T(4,128)} %copy.219), calls=%async_computation.8 | async-start | bytes 1048576 | tf_op jit(solution)/shard_map/all_to_all | solution.py:58
  178.0 7.4 %all-to-all-done.8 = f32[2,4,128,128]{3,1,0,2:T(4,128)S(1)} async-done(((f32[2,4,128,128]{3,1,0,2:T(4,128)}), f32[2,4,128,128]{3,1,0,2:T(4,128)S(1)}, u32[]{:S(2)}, u32[]{:S(2)}) %all-to-all-start.8) | async-done | bytes 524320 | tf_op jit(solution)/shard_map/all_to_all | solution.py:58
  185.6 0.3 copy.221
  185.9 0.7 convolution_bitcast_fusion.3
  186.6 0.7 convolution_bitcast_fusion.2
  187.5 0.3 copy.224
  187.8 13.1 %all_to_all.203 = f32[2,64,8,128]{3,2,0,1:T(8,128)S(1)} all-to-all(f32[2,64,8,128]{3,2,0,1:T(8,128)S(1)} %copy.224), channel_id=1, replica_groups=mesh['trial'=2,'qa'=16,'qb'=8] {'qa'}, dimensions={1} | all-to-all | bytes 1048576 | tf_op jit(solution)/shard_map/all_to_all | solution.py:60
  200.9 1.0 copy.227
  201.9 3.5 %all-to-all-start.10 = ((f32[2,4,128,128]{2,1,0,3:T(4,128)}), f32[2,4,128,128]{2,1,0,3:T(4,128)S(1)}, u32[]{:S(2)}, u32[]{:S(2)}) async-start(f32[2,4,128,128]{2,1,0,3:T(4,128)} %copy.227), calls=%async_computation.10 | async-start | bytes 1048576 | tf_op jit(solution)/shard_map/all_to_all | solution.py:61
  206.9 12.3 %all-to-all-done.10 = f32[2,4,128,128]{2,1,0,3:T(4,128)S(1)} async-done(((f32[2,4,128,128]{2,1,0,3:T(4,128)}), f32[2,4,128,128]{2,1,0,3:T(4,128)S(1)}, u32[]{:S(2)}, u32[]{:S(2)}) %all-to-all-start.10) | async-done | bytes 524320 | tf_op jit(solution)/shard_map/all_to_all | solution.py:61
  219.3 0.9 convolution_bitcast_fusion.1
  220.1 0.9 convolution_bitcast_fusion
  221.3 15.7 %all_to_all.204 = f32[2,32,128,16]{2,3,0,1:T(8,128)S(1)} all-to-all(f32[2,32,128,16]{2,3,0,1:T(8,128)S(1)} %copy.234), channel_id=1, replica_groups=mesh['trial'=2,'qa'=16,'qb'=8] {'qb'}, dimensions={1} | all-to-all | bytes 1048576 | tf_op jit(solution)/shard_map/all_to_all | solution.py:64
  237.1 1.0 copy.237
  (57 shorter events, 3.1 us)
Async XLA Ops:
  3.1 0.7 copy-start.1
  12.3 17.6 %all-to-all-start = ((f32[2,4,128,128]{3,1,0,2:T(4,128)}), f32[2,4,128,128]{3,1,0,2:T(4,128)S(1)}, u32[]{:S(2)}, u32[]{:S(2)}) async-start(f32[2,4,128,128]{3,1,0,2:T(4,128)} %copy.169), calls=%async_computation | async-start | bytes 1048576 | tf_op jit(solution)/shard_map/all_to_all | solution.py:58
  47.0 24.1 %all-to-all-start.2 = ((f32[2,4,128,128]{2,1,0,3:T(4,128)}), f32[2,4,128,128]{2,1,0,3:T(4,128)S(1)}, u32[]{:S(2)}, u32[]{:S(2)}) async-start(f32[2,4,128,128]{2,1,0,3:T(4,128)} %copy.177), calls=%async_computation.2 | async-start | bytes 1048576 | tf_op jit(solution)/shard_map/all_to_all | solution.py:61
  74.1 17.5 %all-to-all-start.3 = ((f32[2,32,128,16]{2,3,0,1:T(8,128)}), f32[2,32,128,16]{2,3,0,1:T(8,128)S(1)}, u32[]{:S(2)}, u32[]{:S(2)}) async-start(f32[2,32,128,16]{2,3,0,1:T(8,128)} %copy.184), calls=%async_computation.3 | async-start | bytes 1048576 | tf_op jit(solution)/shard_map/all_to_all | solution.py:64
  91.8 1.0 copy-start
  98.7 13.8 %all-to-all-start.4 = ((f32[2,4,128,128]{3,1,0,2:T(4,128)}), f32[2,4,128,128]{3,1,0,2:T(4,128)S(1)}, u32[]{:S(2)}, u32[]{:S(2)}) async-start(f32[2,4,128,128]{3,1,0,2:T(4,128)} %copy.194), calls=%async_computation.4 | async-start | bytes 1048576 | tf_op jit(solution)/shard_map/all_to_all | solution.py:58
  129.1 16.7 %all-to-all-start.6 = ((f32[2,4,128,128]{2,1,0,3:T(4,128)}), f32[2,4,128,128]{2,1,0,3:T(4,128)S(1)}, u32[]{:S(2)}, u32[]{:S(2)}) async-start(f32[2,4,128,128]{2,1,0,3:T(4,128)} %copy.202), calls=%async_computation.6 | async-start | bytes 1048576 | tf_op jit(solution)/shard_map/all_to_all | solution.py:61
  148.7 16.7 %all-to-all-start.7 = ((f32[2,32,128,16]{2,3,0,1:T(8,128)}), f32[2,32,128,16]{2,3,0,1:T(8,128)S(1)}, u32[]{:S(2)}, u32[]{:S(2)}) async-start(f32[2,32,128,16]{2,3,0,1:T(8,128)} %copy.209), calls=%async_computation.7 | async-start | bytes 1048576 | tf_op jit(solution)/shard_map/all_to_all | solution.py:64
  171.8 13.7 %all-to-all-start.8 = ((f32[2,4,128,128]{3,1,0,2:T(4,128)}), f32[2,4,128,128]{3,1,0,2:T(4,128)S(1)}, u32[]{:S(2)}, u32[]{:S(2)}) async-start(f32[2,4,128,128]{3,1,0,2:T(4,128)} %copy.219), calls=%async_computation.8 | async-start | bytes 1048576 | tf_op jit(solution)/shard_map/all_to_all | solution.py:58
  201.9 17.3 %all-to-all-start.10 = ((f32[2,4,128,128]{2,1,0,3:T(4,128)}), f32[2,4,128,128]{2,1,0,3:T(4,128)S(1)}, u32[]{:S(2)}, u32[]{:S(2)}) async-start(f32[2,4,128,128]{2,1,0,3:T(4,128)} %copy.227), calls=%async_computation.10 | async-start | bytes 1048576 | tf_op jit(solution)/shard_map/all_to_all | solution.py:61
where the time goes:
time: 239 us; the launch traced here: 238 us
  waiting for transfers between devices  83.1 us (35%)
  blocking collectives  55.6 us (23%)
  starting transfers between devices  40.2 us (17%)
  matrix products  20.9 us (9%)
  between operations  17.6 us (7%)
  local copies, waits for them, and re-layouts  15.4 us (6%)
  other arithmetic  5.26 us (2%)
    all_to_all x3, blocking collectives, shards(): lax.all_to_all(moved, 'qa', split_axis=1, concat_axis=2, tiled=True)  39.9 us
    all_to_all x3, waiting for transfers between devices, shards(): lax.all_to_all(values, 'qb', split_axis=3, concat_axis=1, tiled=True)  38.4 us
    all_to_all x3, waiting for transfers between devices, shards(): lax.all_to_all(values, 'qa', split_axis=2, concat_axis=1, tiled=True)  23.4 us
    all_to_all x2, waiting for transfers between devices, shards(): lax.all_to_all(moved, 'qb', split_axis=1, concat_axis=3, tiled=True)  21.3 us
    dot_general x24, matrix products, times(): jnp.tensordot(values, table, axes=([dim], [0]), precision=lax.Precision.H...  20.9 us
    all_to_all x3, starting transfers between devices, shards(): lax.all_to_all(values, 'qa', split_axis=2, concat_axis=1, tiled=True)  17.4 us
    all_to_all x1, blocking collectives, shards(): lax.all_to_all(moved, 'qb', split_axis=1, concat_axis=3, tiled=True)  15.7 us
    all_to_all x3, starting transfers between devices, shards(): lax.all_to_all(values, 'qb', split_axis=3, concat_axis=1, tiled=True)  15.4 us
  transfers between devices with their start and end apart: 8, of which 8 were waited for; matrix products, arithmetic and copies ran while one was open for 0% of the time, Pallas kernels for 0%

commit v1 on v0

--- a/solution.py
+++ b/solution.py
@@ -61,7 +61,10 @@
         moved = lax.all_to_all(values, "qb", split_axis=3, concat_axis=1, tiled=True)
         spread = moved.reshape(2, lax.axis_size("qb"), -1, moved.shape[2], moved.shape[3])
         moved = mix_dim(spread, 1, turn_angles[layer, 3]).reshape(moved.shape)
-        values = lax.all_to_all(moved, "qb", split_axis=1, concat_axis=3, tiled=True)
+        values = jnp.concatenate(
+            lax.all_to_all(jnp.stack(jnp.split(moved, lax.axis_size("qb"), axis=1)), "qb", 0, 0),
+            axis=3,
+        )
     return values
 
 

time: 239 us -> 248 us (1.038)
  other arithmetic: 5.26 us -> 15.4 us
    unnamed x0 -> x21, other arithmetic: none -> 8.93 us
    another operation x9 -> x6, local copies, waits for them, and re-layouts: 5.69 us -> 3.91 us  [mix_dim(): return jnp.stack([by_real[0] - by_imag[1], by_real[1] + by_imag[0]])]
where the time goes in v1:
time: 248 us; the launch traced here: 247 us
  waiting for transfers between devices  83.5 us (34%)
  blocking collectives  55.7 us (22%)
  starting transfers between devices  40.2 us (16%)
  matrix products  20.9 us (8%)
  between operations  17.6 us (7%)
  other arithmetic  15.4 us (6%)
  local copies, waits for them, and re-layouts  13.6 us (5%)
    all_to_all x3, blocking collectives, shards(): lax.all_to_all(moved, 'qa', split_axis=1, concat_axis=2, tiled=True)  39.9 us
    all_to_all x3, waiting for transfers between devices, shards(): lax.all_to_all(values, 'qb', split_axis=3, concat_axis=1, tiled=True)  38.7 us
    all_to_all x3, waiting for transfers between devices, shards(): lax.all_to_all(values, 'qa', split_axis=2, concat_axis=1, tiled=True)  23.5 us
    all_to_all x2, waiting for transfers between devices, shards(): lax.all_to_all(jnp.stack(jnp.split(moved, lax.axis_size('qb'), axis=1)),...  21.3 us
    dot_general x24, matrix products, times(): jnp.tensordot(values, table, axes=([dim], [0]), precision=lax.Precision.H...  20.9 us
    all_to_all x3, starting transfers between devices, shards(): lax.all_to_all(values, 'qa', split_axis=2, concat_axis=1, tiled=True)  17.3 us
    all_to_all x1, blocking collectives, shards(): lax.all_to_all(jnp.stack(jnp.split(moved, lax.axis_size('qb'), axis=1)),...  15.8 us
    all_to_all x3, starting transfers between devices, shards(): lax.all_to_all(values, 'qb', split_axis=3, concat_axis=1, tiled=True)  15.4 us
  transfers between devices with their start and end apart: 8, of which 8 were waited for; matrix products, arithmetic and copies ran while one was open for 0% of the time, Pallas kernels for 0%

profile of v1, /device:TPU:2, one launch (start us, length us, event | category | flops | bytes accessed | tf_op | source)
XLA Modules:
  0.0 246.8 jit_solution(2366360164211526729)
XLA Ops:
  0.0 1.8 fusion.396
  3.8 2.0 fusion.19
  5.9 0.8 fusion.17
  6.7 0.8 fusion.16
  9.0 1.1 convolution_bitcast_fusion.17
  10.1 1.1 convolution_bitcast_fusion.16
  11.3 1.0 copy.178
  12.3 7.5 %all-to-all-start = ((f32[2,4,128,128]{3,1,0,2:T(4,128)}), f32[2,4,128,128]{3,1,0,2:T(4,128)S(1)}, u32[]{:S(2)}, u32[]{:S(2)}) async-start(f32[2,4,128,128]{3,1,0,2:T(4,128)} %copy.178), calls=%async_computation | async-start | bytes 1048576 | tf_op jit(solution)/shard_map/all_to_all | solution.py:58
  21.3 8.6 %all-to-all-done = f32[2,4,128,128]{3,1,0,2:T(4,128)S(1)} async-done(((f32[2,4,128,128]{3,1,0,2:T(4,128)}), f32[2,4,128,128]{3,1,0,2:T(4,128)S(1)}, u32[]{:S(2)}, u32[]{:S(2)}) %all-to-all-start) | async-done | bytes 524320 | tf_op jit(solution)/shard_map/all_to_all | solution.py:58
  30.4 0.7 convolution_bitcast_fusion.15
  31.1 0.7 convolution_bitcast_fusion.14
  32.3 13.8 %all_to_all.168 = f32[2,64,8,128]{3,2,0,1:T(8,128)S(1)} all-to-all(f32[2,64,8,128]{3,2,0,1:T(8,128)S(1)} %copy.183), channel_id=1, replica_groups=mesh['trial'=2,'qa'=16,'qb'=8] {'qa'}, dimensions={1} | all-to-all | bytes 1048576 | tf_op jit(solution)/shard_map/all_to_all | solution.py:60
  46.1 1.0 copy.186
  47.0 8.5 %all-to-all-start.2 = ((f32[2,4,128,128]{2,1,0,3:T(4,128)}), f32[2,4,128,128]{2,1,0,3:T(4,128)S(1)}, u32[]{:S(2)}, u32[]{:S(2)}) async-start(f32[2,4,128,128]{2,1,0,3:T(4,128)} %copy.186), calls=%async_computation.2 | async-start | bytes 1048576 | tf_op jit(solution)/shard_map/all_to_all | solution.py:61
  57.0 14.2 %all-to-all-done.2 = f32[2,4,128,128]{2,1,0,3:T(4,128)S(1)} async-done(((f32[2,4,128,128]{2,1,0,3:T(4,128)}), f32[2,4,128,128]{2,1,0,3:T(4,128)S(1)}, u32[]{:S(2)}, u32[]{:S(2)}) %all-to-all-start.2) | async-done | bytes 524320 | tf_op jit(solution)/shard_map/all_to_all | solution.py:61
  71.2 0.9 convolution_bitcast_fusion.13
  72.1 0.9 convolution_bitcast_fusion.12
  73.2 0.6 fusion.70
  73.8 0.6 fusion.73
  74.4 0.6 fusion.76
  75.1 0.6 fusion.79
  75.7 0.6 fusion.82
  76.3 0.6 fusion.85
  77.6 0.6 fusion.91
  78.2 3.7 %all-to-all-start.3 = ((f32[8,2,4,128,16]{3,4,2,1,0:T(8,128)}), f32[8,2,4,128,16]{3,4,2,1,0:T(8,128)S(1)}, u32[]{:S(2)}, u32[]{:S(2)}) async-start(f32[8,2,4,128,16]{3,4,2,1,0:T(8,128)} %fusion.91), calls=%async_computation.3 | async-start | bytes 1048576 | tf_op jit(solution)/shard_map/all_to_all | solution.py:65
  84.6 11.2 %all-to-all-done.3 = f32[8,2,4,128,16]{3,4,2,1,0:T(8,128)S(1)} async-done(((f32[8,2,4,128,16]{3,4,2,1,0:T(8,128)}), f32[8,2,4,128,16]{3,4,2,1,0:T(8,128)S(1)}, u32[]{:S(2)}, u32[]{:S(2)}) %all-to-all-start.3) | async-done | bytes 524320 | tf_op jit(solution)/shard_map/all_to_all | solution.py:65
  96.1 0.8 copy-done
  96.9 1.0 add_bitcast_fusion.1
  97.9 0.8 fusion.15
  98.7 0.8 fusion.14
  99.6 1.1 convolution_bitcast_fusion.11
  100.7 1.1 convolution_bitcast_fusion.10
  101.9 1.0 copy.201
  102.9 5.0 %all-to-all-start.4 = ((f32[2,4,128,128]{3,1,0,2:T(4,128)}), f32[2,4,128,128]{3,1,0,2:T(4,128)S(1)}, u32[]{:S(2)}, u32[]{:S(2)}) async-start(f32[2,4,128,128]{3,1,0,2:T(4,128)} %copy.201), calls=%async_computation.4 | async-start | bytes 1048576 | tf_op jit(solution)/shard_map/all_to_all | solution.py:58
  109.3 7.4 %all-to-all-done.4 = f32[2,4,128,128]{3,1,0,2:T(4,128)S(1)} async-done(((f32[2,4,128,128]{3,1,0,2:T(4,128)}), f32[2,4,128,128]{3,1,0,2:T(4,128)S(1)}, u32[]{:S(2)}, u32[]{:S(2)}) %all-to-all-start.4) | async-done | bytes 524320 | tf_op jit(solution)/shard_map/all_to_all | solution.py:58
  117.2 0.7 convolution_bitcast_fusion.9
  118.0 0.7 convolution_bitcast_fusion.8
  119.1 13.1 %all_to_all.169 = f32[2,64,8,128]{3,2,0,1:T(8,128)S(1)} all-to-all(f32[2,64,8,128]{3,2,0,1:T(8,128)S(1)} %copy.206), channel_id=1, replica_groups=mesh['trial'=2,'qa'=16,'qb'=8] {'qa'}, dimensions={1} | all-to-all | bytes 1048576 | tf_op jit(solution)/shard_map/all_to_all | solution.py:60
  132.3 1.0 copy.209
  133.2 3.5 %all-to-all-start.6 = ((f32[2,4,128,128]{2,1,0,3:T(4,128)}), f32[2,4,128,128]{2,1,0,3:T(4,128)S(1)}, u32[]{:S(2)}, u32[]{:S(2)}) async-start(f32[2,4,128,128]{2,1,0,3:T(4,128)} %copy.209), calls=%async_computation.6 | async-start | bytes 1048576 | tf_op jit(solution)/shard_map/all_to_all | solution.py:61
  138.0 11.9 %all-to-all-done.6 = f32[2,4,128,128]{2,1,0,3:T(4,128)S(1)} async-done(((f32[2,4,128,128]{2,1,0,3:T(4,128)}), f32[2,4,128,128]{2,1,0,3:T(4,128)S(1)}, u32[]{:S(2)}, u32[]{:S(2)}) %all-to-all-start.6) | async-done | bytes 524320 | tf_op jit(solution)/shard_map/all_to_all | solution.py:61
  150.0 0.9 convolution_bitcast_fusion.7
  150.8 0.9 convolution_bitcast_fusion.6
  151.9 0.6 fusion.49
  157.0 3.7 %all-to-all-start.7 = ((f32[8,2,4,128,16]{3,4,2,1,0:T(8,128)}), f32[8,2,4,128,16]{3,4,2,1,0:T(8,128)S(1)}, u32[]{:S(2)}, u32[]{:S(2)}) async-start(f32[8,2,4,128,16]{3,4,2,1,0:T(8,128)} %fusion.89), calls=%async_computation.7 | async-start | bytes 1048576 | tf_op jit(solution)/shard_map/all_to_all | solution.py:65
  163.6 10.1 %all-to-all-done.7 = f32[8,2,4,128,16]{3,4,2,1,0:T(8,128)S(1)} async-done(((f32[8,2,4,128,16]{3,4,2,1,0:T(8,128)}), f32[8,2,4,128,16]{3,4,2,1,0:T(8,128)S(1)}, u32[]{:S(2)}, u32[]{:S(2)}) %all-to-all-start.7) | async-done | bytes 524320 | tf_op jit(solution)/shard_map/all_to_all | solution.py:65
  174.1 1.0 add_bitcast_fusion
  175.1 0.8 fusion.13
  175.9 0.8 fusion.12
  176.8 1.1 convolution_bitcast_fusion.5
  177.9 1.1 convolution_bitcast_fusion.4
  179.1 1.0 copy.224
  180.1 4.8 %all-to-all-start.8 = ((f32[2,4,128,128]{3,1,0,2:T(4,128)}), f32[2,4,128,128]{3,1,0,2:T(4,128)S(1)}, u32[]{:S(2)}, u32[]{:S(2)}) async-start(f32[2,4,128,128]{3,1,0,2:T(4,128)} %copy.224), calls=%async_computation.8 | async-start | bytes 1048576 | tf_op jit(solution)/shard_map/all_to_all | solution.py:58
  186.3 7.4 %all-to-all-done.8 = f32[2,4,128,128]{3,1,0,2:T(4,128)S(1)} async-done(((f32[2,4,128,128]{3,1,0,2:T(4,128)}), f32[2,4,128,128]{3,1,0,2:T(4,128)S(1)}, u32[]{:S(2)}, u32[]{:S(2)}) %all-to-all-start.8) | async-done | bytes 524320 | tf_op jit(solution)/shard_map/all_to_all | solution.py:58
  194.2 0.7 convolution_bitcast_fusion.3
  194.9 0.7 convolution_bitcast_fusion.2
  196.1 13.1 %all_to_all.170 = f32[2,64,8,128]{3,2,0,1:T(8,128)S(1)} all-to-all(f32[2,64,8,128]{3,2,0,1:T(8,128)S(1)} %copy.229), channel_id=1, replica_groups=mesh['trial'=2,'qa'=16,'qb'=8] {'qa'}, dimensions={1} | all-to-all | bytes 1048576 | tf_op jit(solution)/shard_map/all_to_all | solution.py:60
  209.2 1.0 copy.232
  210.2 3.5 %all-to-all-start.10 = ((f32[2,4,128,128]{2,1,0,3:T(4,128)}), f32[2,4,128,128]{2,1,0,3:T(4,128)S(1)}, u32[]{:S(2)}, u32[]{:S(2)}) async-start(f32[2,4,128,128]{2,1,0,3:T(4,128)} %copy.232), calls=%async_computation.10 | async-start | bytes 1048576 | tf_op jit(solution)/shard_map/all_to_all | solution.py:61
  215.3 12.7 %all-to-all-done.10 = f32[2,4,128,128]{2,1,0,3:T(4,128)S(1)} async-done(((f32[2,4,128,128]{2,1,0,3:T(4,128)}), f32[2,4,128,128]{2,1,0,3:T(4,128)S(1)}, u32[]{:S(2)}, u32[]{:S(2)}) %all-to-all-start.10) | async-done | bytes 524320 | tf_op jit(solution)/shard_map/all_to_all | solution.py:61
  227.9 0.9 convolution_bitcast_fusion.1
  228.8 0.9 convolution_bitcast_fusion
  230.0 15.8 %all_to_all.171 = f32[8,2,4,128,16]{3,4,2,1,0:T(8,128)S(1)} all-to-all(f32[8,2,4,128,16]{3,4,2,1,0:T(8,128)S(1)} %fusion.87), channel_id=1, replica_groups=mesh['trial'=2,'qa'=16,'qb'=8] {'qb'}, dimensions={0} | all-to-all | bytes 1048576 | tf_op jit(solution)/shard_map/all_to_all | solution.py:65
  245.8 1.0 copy.240
  (73 shorter events, 10.2 us)
Async XLA Ops:
  3.1 0.7 copy-start.1
  12.3 17.6 %all-to-all-start = ((f32[2,4,128,128]{3,1,0,2:T(4,128)}), f32[2,4,128,128]{3,1,0,2:T(4,128)S(1)}, u32[]{:S(2)}, u32[]{:S(2)}) async-start(f32[2,4,128,128]{3,1,0,2:T(4,128)} %copy.178), calls=%async_computation | async-start | bytes 1048576 | tf_op jit(solution)/shard_map/all_to_all | solution.py:58
  47.0 24.1 %all-to-all-start.2 = ((f32[2,4,128,128]{2,1,0,3:T(4,128)}), f32[2,4,128,128]{2,1,0,3:T(4,128)S(1)}, u32[]{:S(2)}, u32[]{:S(2)}) async-start(f32[2,4,128,128]{2,1,0,3:T(4,128)} %copy.186), calls=%async_computation.2 | async-start | bytes 1048576 | tf_op jit(solution)/shard_map/all_to_all | solution.py:61
  78.2 17.5 %all-to-all-start.3 = ((f32[8,2,4,128,16]{3,4,2,1,0:T(8,128)}), f32[8,2,4,128,16]{3,4,2,1,0:T(8,128)S(1)}, u32[]{:S(2)}, u32[]{:S(2)}) async-start(f32[8,2,4,128,16]{3,4,2,1,0:T(8,128)} %fusion.91), calls=%async_computation.3 | async-start | bytes 1048576 | tf_op jit(solution)/shard_map/all_to_all | solution.py:65
  96.0 1.0 copy-start
  102.9 13.9 %all-to-all-start.4 = ((f32[2,4,128,128]{3,1,0,2:T(4,128)}), f32[2,4,128,128]{3,1,0,2:T(4,128)S(1)}, u32[]{:S(2)}, u32[]{:S(2)}) async-start(f32[2,4,128,128]{3,1,0,2:T(4,128)} %copy.201), calls=%async_computation.4 | async-start | bytes 1048576 | tf_op jit(solution)/shard_map/all_to_all | solution.py:58
  133.2 16.7 %all-to-all-start.6 = ((f32[2,4,128,128]{2,1,0,3:T(4,128)}), f32[2,4,128,128]{2,1,0,3:T(4,128)S(1)}, u32[]{:S(2)}, u32[]{:S(2)}) async-start(f32[2,4,128,128]{2,1,0,3:T(4,128)} %copy.209), calls=%async_computation.6 | async-start | bytes 1048576 | tf_op jit(solution)/shard_map/all_to_all | solution.py:61
  157.0 16.7 %all-to-all-start.7 = ((f32[8,2,4,128,16]{3,4,2,1,0:T(8,128)}), f32[8,2,4,128,16]{3,4,2,1,0:T(8,128)S(1)}, u32[]{:S(2)}, u32[]{:S(2)}) async-start(f32[8,2,4,128,16]{3,4,2,1,0:T(8,128)} %fusion.89), calls=%async_computation.7 | async-start | bytes 1048576 | tf_op jit(solution)/shard_map/all_to_all | solution.py:65
  180.1 13.7 %all-to-all-start.8 = ((f32[2,4,128,128]{3,1,0,2:T(4,128)}), f32[2,4,128,128]{3,1,0,2:T(4,128)S(1)}, u32[]{:S(2)}, u32[]{:S(2)}) async-start(f32[2,4,128,128]{3,1,0,2:T(4,128)} %copy.224), calls=%async_computation.8 | async-start | bytes 1048576 | tf_op jit(solution)/shard_map/all_to_all | solution.py:58
  210.2 17.7 %all-to-all-start.10 = ((f32[2,4,128,128]{2,1,0,3:T(4,128)}), f32[2,4,128,128]{2,1,0,3:T(4,128)S(1)}, u32[]{:S(2)}, u32[]{:S(2)}) async-start(f32[2,4,128,128]{2,1,0,3:T(4,128)} %copy.232), calls=%async_computation.10 | async-start | bytes 1048576 | tf_op jit(solution)/shard_map/all_to_all | solution.py:61
